TPU v7x, 768 devices: a whole 4x8x12 slice. The times are simulated.
768 devices in a mesh: dp: 32 (over z_hi, x, core), tensor: 24 (over z_lo, y).
Axes of the slice: x: 4, y: 8, z: 12 (z_hi: 4, z_lo: 3; z = z_hi * 3 + z_lo), core: 2. Of those that a mesh axis runs over, the one named last changes fastest.
Arguments:
- saved_input: bfloat16 [8192, 6144], P('dp', 'tensor'), may hold values from -6 to 6
- queries: bfloat16 [8192, 6144], P('dp', 'tensor'), may hold values from -8 to 8
- keys: bfloat16 [8192, 6144], P('dp', 'tensor'), may hold values from -8 to 8
- value_weight: bfloat16 [6144, 6144], P(None, 'tensor'), may hold values from -0.125 to 0.125
- grad_attended: bfloat16 [8192, 6144], P('dp', 'tensor'), may hold values from -6 to 6
Outputs:
- grad_input: bfloat16 [8192, 6144], P('dp', 'tensor')
- grad_value_weight: float32 [6144, 6144], P('dp', 'tensor')
- grad_queries: bfloat16 [8192, 6144], P('dp', 'tensor')
- grad_keys: bfloat16 [8192, 6144], P('dp', 'tensor')
All inputs are finite; a program needn't handle non-finite values.
Results may differ from a plain program's by a relative error of at most 0.02.
Values may be sent and summed in bfloat16 or wider, within the bound.
A program may use at most 64 MiB of HBM per device.

v0:
```python
import jax
import jax.numpy as jnp
from jax import lax
from jax.sharding import Mesh
from jax.sharding import PartitionSpec as P

HD = 128
TENSOR = ("tensor_0", "tensor_1")


def in_order(pieces, dim):
    pieces = jnp.moveaxis(pieces, 0, dim)
    shape = pieces.shape
    return pieces.reshape(*shape[:dim], shape[dim] * shape[dim + 1], *shape[dim + 2 :])


def all_blocks(shard, axes, sequence):
    pieces = shard[None]
    for k in sequence:
        pieces = lax.all_gather(pieces, axes[k], axis=0, tiled=True)
    block = [lax.axis_size(axes[k]) for k in reversed(sequence)]
    pieces = pieces.reshape(*block, *shard.shape)
    turned = sorted(range(len(sequence)), key=lambda place: sequence[len(sequence) - 1 - place])
    return pieces.transpose(*turned, *range(len(sequence), pieces.ndim)).reshape(-1, *shard.shape)


def gathered_by_axis(shard, axes, sequence, dim):
    return in_order(all_blocks(shard, axes, sequence), dim)


def own_block(pieces, axes, sequence):
    inside = pieces.shape[1:]
    pieces = pieces.reshape(*(lax.axis_size(a) for a in axes), *inside)
    pieces = jnp.moveaxis(pieces, sequence, range(len(axes))).reshape(-1, *inside)
    for k in sequence:
        pieces = lax.psum_scatter(pieces, axes[k], scatter_dimension=0, tiled=True)
    return pieces[0]


def in_blocks(shard, dim, count):
    before, after = (shard.shape[:dim], shard.shape[dim + 1 :])
    return jnp.moveaxis(shard.reshape(*before, count, -1, *after), dim, 0)


def sum_by_axis(shard, axes, sequence, dim):
    count = lax.axis_size(axes)
    return own_block(in_blocks(shard, dim, count), axes, sequence)


def on_device(saved_input, queries, keys, value_weight, grad_attended):
    token_count = queries.shape[0]
    local_width = value_weight.shape[1]
    local_heads = local_width // HD
    score_scale = 1.0 / jnp.sqrt(jnp.float32(HD))
    full_input = gathered_by_axis(saved_input, TENSOR, (0, 1), 1)
    values = jnp.dot(full_input, value_weight, preferred_element_type=jnp.float32).astype(
        jnp.bfloat16
    )
    query_heads = queries.reshape(token_count, local_heads, HD)
    key_heads = keys.reshape(token_count, local_heads, HD)
    value_heads = values.reshape(token_count, local_heads, HD)
    grad_heads = grad_attended.reshape(token_count, local_heads, HD)
    scores = (
        jnp.einsum("qhd,khd->hqk", query_heads, key_heads, preferred_element_type=jnp.float32)
        * score_scale
    )
    positions = lax.iota(jnp.int32, token_count)
    causal = positions[:, None] >= positions[None, :]
    scores = jnp.where(causal[None], scores, -jnp.inf)
    row_max = jnp.max(scores, axis=-1, keepdims=True)
    weights_exp = jnp.exp(scores - row_max)
    attention = weights_exp / jnp.sum(weights_exp, axis=-1, keepdims=True)
    probs_half = attention.astype(jnp.bfloat16)
    grad_values = jnp.einsum(
        "hqk,qhd->khd", probs_half, grad_heads, preferred_element_type=jnp.float32
    ).astype(jnp.bfloat16)
    grad_probs = jnp.einsum(
        "qhd,khd->hqk", grad_heads, value_heads, preferred_element_type=jnp.float32
    )
    row_dot = jnp.sum(attention * grad_probs, axis=-1, keepdims=True)
    grad_scores = (attention * (grad_probs - row_dot) * score_scale).astype(jnp.bfloat16)
    grad_queries = jnp.einsum(
        "hqk,khd->qhd", grad_scores, key_heads, preferred_element_type=jnp.float32
    ).astype(jnp.bfloat16)
    grad_keys = jnp.einsum(
        "hqk,qhd->khd", grad_scores, query_heads, preferred_element_type=jnp.float32
    ).astype(jnp.bfloat16)
    value_flat = grad_values.reshape(token_count, local_width)
    data_groups = lax.axis_size("dp")
    partial_value = lax.dot_general(
        value_flat, value_weight, (((1,), (1,)), ((), ())), preferred_element_type=jnp.float32
    )
    grad_input = (
        sum_by_axis(partial_value.astype(jnp.bfloat16), TENSOR, (1, 0), 1)
        .astype(jnp.float32)
        .astype(jnp.bfloat16)
    )
    partial_value = lax.dot_general(
        full_input, value_flat, (((0,), (0,)), ((), ())), preferred_element_type=jnp.float32
    )
    summed = lax.psum_scatter(
        partial_value.astype(jnp.bfloat16), "dp", scatter_dimension=0, tiled=True
    ).astype(jnp.float32)
    grad_value_weight = summed / jnp.float32(data_groups)
    return (
        grad_input,
        grad_value_weight,
        grad_queries.reshape(token_count, local_width),
        grad_keys.reshape(token_count, local_width),
    )


def solution(mesh):
    torus = Mesh(mesh.devices.reshape(mesh.shape["dp"], 3, 8), ("dp", "tensor_0", "tensor_1"))
    placed = (P("dp", TENSOR), P("dp", TENSOR), P("dp", TENSOR), P(None, TENSOR), P("dp", TENSOR))
    return jax.shard_map(
        on_device,
        mesh=torus,
        in_specs=placed,
        out_specs=(P("dp", TENSOR), P("dp", TENSOR), P("dp", TENSOR), P("dp", TENSOR)),
        check_vma=False,
    )
```

profile of v0, /device:TPU:1, one launch (start us, length us, event | category | flops | bytes accessed | tf_op | source)
XLA Modules:
  0.0 291.2 jit_solution(5928817438978503912)
XLA Ops:
  7.2 0.0 all-gather.3.cloned.1.call-start
  7.2 12.0 %all-gather = bf16[768,256]{1,0:T(8,128)(2,1)} all-gather(bf16[256,256]{1,0:T(8,128)(2,1)} %param.5), channel_id=2, replica_groups=mesh['dp'=32,'tensor_0'=3,'tensor_1'=8] {'tensor_0'}, dimensions={0}, use_global_device_ids=true | all-gather | bytes 524288 | tf_op jit(solution)/shard_map/all_gather | solution.py:20
  19.2 0.0 all-gather.3.cloned.1.call-update
  19.2 0.0 reduce-scatter.6.cloned.1.call-start
  19.3 1.0 copy.76
  20.3 1.0 copy.77
  21.3 1.2 fusion.28
  22.5 1.5 convolution_convert_fusion.4
  24.1 1.0 convolution_convert_fusion.1
  25.1 1.0 copy.79
  26.1 2.4 copy.58
  28.5 0.0 reduce-scatter.6.cloned.1.call-update
  28.5 0.0 reduce-scatter.10.cloned.1.call-start
  28.6 48.5 %all-gather.3.cloned.1.call-done = bf16[24,256,256]{2,1,0:T(8,128)(2,1)} async-done(((bf16[3,256,256]{2,1,0:T(8,128)(2,1)}), bf16[24,256,256]{2,1,0:T(8,128)(2,1)}) %all-gather.3.cloned.1.call-update) | async-done | bytes 3145744 | tf_op jit(solution)/shard_map/all_gather | solution.py:20
  77.1 3.8 %copy.59 = bf16[3,8,256,256]{3,2,1,0:T(8,128)(2,1)} copy(bf16[3,8,256,256]{3,2,0,1:T(8,128)(2,1)} %bitcast.66) | data formatting | bytes 6291456 | tf_op jit(solution)/shard_map/transpose | solution.py:24
  80.9 4.7 %copy.60 = bf16[256,24,256]{0,2,1:T(8,128)(2,1)} copy(bf16[256,24,256]{2,0,1:T(8,128)(2,1)} %bitcast.64) | data formatting | bytes 6291456 | tf_op jit(solution)/shard_map/transpose | solution.py:12
  85.6 4.5 %fusion.2 = bf16[6144,256]{0,1:T(8,128)(2,1)} fusion(bf16[256,256]{0,1:T(8,128)(2,1)S(1)} %bitcast.69, bf16[256,6144]{0,1:T(8,128)(2,1)} %bitcast.61), kind=kOutput, calls=%fused_computation.4 | convolution fusion | flops 806879232 | bytes 6422528 | tf_op jit(solution)/shard_map/dot_general | solution.py:98
  90.2 4.7 %copy.74 = bf16[6144,256]{1,0:T(8,128)(2,1)} copy(bf16[6144,256]{0,1:T(8,128)(2,1)} %fusion.2) | data formatting | bytes 6291456
  94.8 0.0 reduce-scatter.10.cloned.1.call-update
  94.9 0.0 reduce-scatter.8.cloned.1.call-start
  94.9 3.9 %convolution_convert_fusion.5 = bf16[256,256]{0,1:T(8,128)(2,1)} fusion(bf16[256,6144]{0,1:T(8,128)(2,1)} %bitcast.62, bf16[6144,256]{1,0:T(8,128)(2,1)S(1)} %copy-done), kind=kOutput, calls=%fused_computation.17 | convolution fusion | flops 805371904 | bytes 6422528 | tf_op jit(solution)/shard_map/dot_general | solution.py:56
  98.8 30.2 %reduce-scatter.6.cloned.1.call-done = bf16[3,256,256]{2,1,0:T(8,128)(2,1)} async-done(((bf16[24,256,256]{2,1,0:T(8,128)(2,1)}), bf16[3,256,256]{2,1,0:T(8,128)(2,1)}) %reduce-scatter.6.cloned.1.call-update) | async-done | bytes 393232 | tf_op jit(solution)/shard_map/reduce_scatter | solution.py:36
  129.0 0.0 reduce-scatter.8.cloned.1.call-update
  129.0 2.0 convolution_bitcast_fusion
  131.0 1.8 convolution_convert_fusion.2
  132.9 0.8 copy.68
  133.6 1.9 convolution_convert_fusion.3
  135.5 0.8 copy.69
  136.2 121.9 %reduce-scatter.10.cloned.1.call-done = bf16[192,256]{1,0:T(8,128)(2,1)} async-done(((bf16[6144,256]{1,0:T(8,128)(2,1)}), bf16[192,256]{1,0:T(8,128)(2,1)}) %reduce-scatter.10.cloned.1.call-update) | async-done | bytes 98320
  258.1 1.0 copy.75
  259.2 0.8 copy.67
  259.9 24.8 %reduce-scatter.8.cloned.1.call-done = bf16[1,256,256]{2,1,0:T(8,128)(2,1)} async-done(((bf16[3,256,256]{2,1,0:T(8,128)(2,1)}), bf16[1,256,256]{2,1,0:T(8,128)(2,1)}) %reduce-scatter.8.cloned.1.call-update) | async-done | bytes 131088 | tf_op jit(solution)/shard_map/reduce_scatter | solution.py:36
  (8 shorter events, 0.1 us)
Async XLA Ops:
  7.2 16.9 %copy-start = (bf16[6144,256]{1,0:T(8,128)(2,1)S(1)}, bf16[6144,256]{1,0:T(8,128)(2,1)}, u32[]{:S(2)}) copy-start(bf16[6144,256]{1,0:T(8,128)(2,1)} %param.8) | copy-start | bytes 9437188
  7.2 69.9 %all-gather.3.cloned.1.call-start = ((), (), s32[]{:S(2)}) async-start(), calls=%async_computation.5 | async-start | bytes 3538944 | tf_op jit(solution)/shard_map/all_gather | solution.py:20
  19.2 109.8 %reduce-scatter.6.cloned.1.call-start = ((), (), s32[]{:S(2)}) async-start(), calls=%async_computation.3 | async-start | bytes 3538944 | tf_op jit(solution)/shard_map/reduce_scatter | solution.py:36
  21.3 1.2 copy-start.2
  28.5 229.6 %reduce-scatter.10.cloned.1.call-start = ((), (), s32[]{:S(2)}) async-start(), calls=%async_computation.6 | async-start | bytes 3244032
  94.9 34.2 %copy-start.1 = (bf16[256,256]{1,0:T(8,128)(2,1)S(1)}, bf16[256,256]{1,0:T(8,128)(2,1)}, u32[]{:S(2)}) copy-start(bf16[256,256]{1,0:T(8,128)(2,1)} %param.9) | copy-start | bytes 393220
  94.9 189.8 %reduce-scatter.8.cloned.1.call-start = ((), (), s32[]{:S(2)}) async-start(), calls=%async_computation.4 | async-start | bytes 524288 | tf_op jit(solution)/shard_map/reduce_scatter | solution.py:36
Sparse Core Ops, SparseCore 0:
  19.3 57.6 all-gather.2
  80.2 48.7 reduce-scatter.5
  134.1 123.9 reduce-scatter.9
  261.7 22.9 reduce-scatter.7
where the time goes:
time: 292 us; the launch traced here: 291 us
  waiting for transfers between devices  225 us (77%)
  local copies, waits for them, and re-layouts  21.9 us (8%)
  matrix products  17.9 us (6%)
  between operations  13.9 us (5%)
  blocking collectives  12 us (4%)
    unnamed x5, waiting for transfers between devices  122 us
    reduce_scatter x2, waiting for transfers between devices, own_block(): pieces = lax.psum_scatter(pieces, axes[k], scatter_dimension=0, tiled=True)  54.9 us
    all_gather x1, waiting for transfers between devices, all_blocks(): pieces = lax.all_gather(pieces, axes[k], axis=0, tiled=True)  48.5 us
    all_gather x1, blocking collectives, all_blocks(): pieces = lax.all_gather(pieces, axes[k], axis=0, tiled=True)  12 us
    unnamed x12, local copies, waits for them, and re-layouts  8.99 us
  transfers between devices with their start and end apart: 4, of which 4 were waited for; matrix products, arithmetic and copies ran while one was open for 14% of the time, Pallas kernels for 0%

commit v1 on v0

v1 whole, which is shorter than its diff:
```python
import math

import jax
import jax.numpy as jnp
from jax import lax
from jax.experimental import pallas as pl
from jax.experimental.pallas import tpu as pltpu
from jax.sharding import Mesh
from jax.sharding import PartitionSpec as P

HD = 128
HEADS = 2
ZH, X, C, ZL, Y = 4, 4, 2, 3, 8
AXES = ("zh", "x", "c", "zl", "y")
T = ZL * Y
B = 256
H = B // 2
MESH = pl.DeviceIdType.MESH
F32 = jnp.float32
BF16 = jnp.bfloat16
SCALE = 1.0 / math.sqrt(HD)


def dot(a, b, ca, cb):
    return lax.dot_general(a, b, (((ca,), (cb,)), ((), ())), preferred_element_type=F32)


def kernel(
    x_hbm, q_hbm, k_hbm, w_hbm, ga_hbm,
    gi_ref, gw_ref, gq_ref, gk_ref,
    xall, w, q, k, ga, gv, att, vals, acc0, acc1,
    wt, crecv, abuf, xr1, xr2, bbuf, zr1, zr2,
    s4_out, s4_in, rs_out, rs_in, tz_out, tz_in,
    in_sem, agz_s, agz_r, ag_s, ag_r, rs_s, rs_r, tz_s, tz_r,
    c_s, c_r, x1_s, x1_r, x2_s, x2_r, z1_s, z1_r, z2_s, z2_r,
):
    zh, xx, c, zl, y = (lax.axis_index(a) for a in AXES)
    me = zl * Y + y
    acc = (acc0, acc1)

    def up(value, step, size):
        return lax.rem(value + (step + size), size)

    ahead = ({"y": up(y, 1, Y)}, {"y": up(y, -1, Y)})
    x_side = ({"x": up(xx, 1, X)}, {"x": up(xx, -1, X)})
    z_side = ({"zh": up(zh, 1, ZH)}, {"zh": up(zh, -1, ZH)})
    plane = ({"zl": up(zl, 1, ZL)}, {"zl": up(zl, 2, ZL)})
    partner = {"c": 1 - c}

    def remote(src, dst, send, recv, where):
        return pltpu.make_async_remote_copy(
            src_ref=src, dst_ref=dst, send_sem=send, recv_sem=recv,
            device_id=where, device_id_type=MESH,
        )

    loads = [
        pltpu.make_async_copy(x_hbm, xall.at[me], in_sem.at[0]),
        pltpu.make_async_copy(q_hbm, q, in_sem.at[1]),
        pltpu.make_async_copy(k_hbm, k, in_sem.at[2]),
        pltpu.make_async_copy(ga_hbm, ga, in_sem.at[3]),
        pltpu.make_async_copy(w_hbm, w, in_sem.at[4]),
    ]
    for load in loads:
        load.start()

    barrier = pltpu.get_barrier_semaphore()
    friends = (*ahead, *x_side, *z_side, *plane, partner)
    for friend in friends:
        pl.semaphore_signal(barrier, inc=1, device_id=friend, device_id_type=MESH)
    pl.semaphore_wait(barrier, len(friends))

    def near(kk):
        return up(zl, -kk, ZL)

    def ag_full(d, s, kk, t):
        return remote(xall.at[t], xall.at[t], ag_s.at[d, s, kk], ag_r.at[d, s, kk], ahead[d])

    def ag_half(d, kk, t):
        part = pl.ds(d * H, H)
        return remote(
            xall.at[t, part], xall.at[t, part], ag_s.at[d, 3, kk], ag_r.at[d, 3, kk], ahead[d]
        )

    def ag_z(j, t):
        return remote(xall.at[t], xall.at[t], agz_s.at[j], agz_r.at[j], plane[j])

    loads[0].wait()
    for j in range(2):
        ag_z(j, me).start()
    for d in range(2):
        ag_full(d, 0, 0, me).start()

    row = lax.broadcasted_iota(jnp.int32, (B, B), 0)
    col = lax.broadcasted_iota(jnp.int32, (B, B), 1)
    for load in loads[1:4]:
        load.wait()

    def probs(h):
        cols = slice(h * HD, (h + 1) * HD)
        scores = dot(q[:, cols], k[:, cols], 1, 1) * SCALE
        scores = jnp.where(row >= col, scores, -jnp.inf)
        e = jnp.exp(scores - jnp.max(scores, axis=-1, keepdims=True))
        a = e / jnp.sum(e, axis=-1, keepdims=True)
        att[h] = a
        gv[:, cols] = dot(a.astype(BF16), ga[:, cols], 0, 0).astype(BF16)

    probs(0)
    for j in range(2):
        t = near(j + 1) * Y + y
        ag_z(j, t).wait_recv()
        for d in range(2):
            ag_full(d, 0, j + 1, t).start()
    probs(1)
    vals[...] = jnp.zeros_like(vals)
    loads[4].wait()

    def consume(t):
        rows = pl.ds(pl.multiple_of(t * B, B), B)
        vals[...] += dot(xall[t], w[rows], 1, 0)
        term = dot(xall[t], gv[...], 0, 0).astype(BF16)
        wt[pl.ds(t * 4, 4)] = term.reshape(4, 64, B)

    def own_chunks(kk, carry):
        consume(near(kk) * Y + y)
        return carry

    lax.fori_loop(0, ZL, own_chunks, 0)

    def ring(i, carry):
        s = i // ZL
        kk = lax.rem(i, ZL)
        ts = (near(kk) * Y + up(y, -(s + 1), Y), near(kk) * Y + up(y, s + 1, Y))
        for d in range(2):
            ag_full(d, s, kk, ts[d]).wait_recv()

            @pl.when(s < 2)
            def _():
                ag_full(d, s + 1, kk, ts[d]).start()

            @pl.when(s == 2)
            def _():
                ag_half(d, kk, ts[d]).start()

        for d in range(2):
            consume(ts[d])
        return carry

    lax.fori_loop(0, 3 * ZL, ring, 0)

    def far(kk):
        return up(zl, kk + 1, ZL)

    def share(t):
        rows = pl.ds(pl.multiple_of(t * B, B), B)
        return dot(gv[...], w[rows], 1, 1)

    def rs_half(d, kk):
        return remote(
            s4_out.at[d, kk], s4_in.at[d, kk], rs_s.at[d, 0, kk], rs_r.at[d, 0, kk], ahead[d]
        )

    def rs_full(d, n, kk):
        return remote(
            rs_out.at[d, n, kk], rs_in.at[d, n, kk],
            rs_s.at[d, n + 1, kk], rs_r.at[d, n + 1, kk], ahead[d],
        )

    def rs_z(j):
        return remote(tz_out.at[j], tz_in.at[j], tz_s.at[j], tz_r.at[j], plane[j])

    def rs_first(kk, carry):
        p = share(far(kk) * Y + up(y, 4, Y)).astype(BF16)
        for d in range(2):
            s4_out[d, kk] = p[d * H : (d + 1) * H]
            rs_half(d, kk).start()
        return carry

    lax.fori_loop(0, ZL, rs_first, 0)

    def last_chunks(kk, carry):
        t = near(kk) * Y + up(y, 4, Y)
        for d in range(2):
            ag_half(d, kk, t).wait_recv()
        consume(t)
        return carry

    lax.fori_loop(0, ZL, last_chunks, 0)

    def c_send(i):
        other = (2 * i + 1 - c) * 3
        return remote(wt.at[pl.ds(other, 3)], crecv.at[i], c_s.at[i], c_r.at[i], partner)

    def x_first(d):
        return remote(
            abuf.at[pl.ds(2 * d, 2), up(xx, 2, X)], xr1.at[d], x1_s.at[d], x1_r.at[d], x_side[d]
        )

    def x_second(d):
        return remote(
            abuf.at[:, x_side[d]["x"]], xr2.at[d], x2_s.at[d], x2_r.at[d], x_side[d]
        )

    def z_first(d):
        return remote(
            bbuf.at[up(zh, 2, ZH), :, pl.ds(32 * d, 32)], zr1.at[d],
            z1_s.at[d], z1_r.at[d], z_side[d],
        )

    def z_second(d):
        return remote(
            bbuf.at[z_side[d]["zh"]], zr2.at[d], z2_s.at[d], z2_r.at[d], z_side[d]
        )

    def cores(i, carry):
        c_send(i).start()
        return carry

    lax.fori_loop(0, ZH * X, cores, 0)

    def pair_sum(j, carry):
        to = up(xx, 2 + j // ZH, X)
        i = lax.rem(j, ZH) * X + to
        c_send(i).wait_recv()
        mine = wt[pl.ds((2 * i + c) * 3, 3)].astype(F32)
        abuf[lax.rem(j, ZH), to] = (mine + crecv[i].astype(F32)).astype(BF16)
        return carry

    lax.fori_loop(0, ZH, pair_sum, 0)
    for d in range(2):
        x_first(d).start()
    lax.fori_loop(ZH, ZH * X, pair_sum, 0)

    def rs_block(n):
        step = 3 - n

        def body(kk, carry):
            for d in range(2):
                acc[d][...] = share(far(kk) * Y + up(y, step if d == 0 else -step, Y))
            for d in range(2):
                if n == 0:
                    rs_half(d, kk).wait_recv()
                    part = slice(d * H, (d + 1) * H)
                    acc[d][part] += s4_in[d, kk].astype(F32)
                    rs_out[d, n, kk] = acc[d][...].astype(BF16)
                else:
                    rs_full(d, n - 1, kk).wait_recv()
                    rs_out[d, n, kk] = (acc[d][...] + rs_in[d, n - 1, kk].astype(F32)).astype(BF16)
                rs_full(d, n, kk).start()
            return carry

        lax.fori_loop(0, ZL, body, 0)

    rs_block(0)

    def grads(h):
        cols = slice(h * HD, (h + 1) * HD)
        a = att[h]
        gp = dot(ga[:, cols], vals[:, cols].astype(BF16), 1, 1)
        rd = jnp.sum(a * gp, axis=-1, keepdims=True)
        gs = (a * (gp - rd) * SCALE).astype(BF16)
        gq_ref[:, cols] = dot(gs, k[:, cols], 1, 0).astype(BF16)
        gk_ref[:, cols] = dot(gs, q[:, cols], 0, 0).astype(BF16)

    for d in range(2):
        x_first(d).wait_recv()
        to = x_side[d]["x"]
        for half in range(2):
            m = 2 * d + half
            abuf[m, to] = (abuf[m, to].astype(F32) + xr1[d, half].astype(F32)).astype(BF16)
        x_second(d).start()

    rs_block(1)
    for d in range(2):
        x_second(d).wait_recv()

    def x_sum(m, carry):
        total = abuf[m, xx].astype(F32) + xr2[0, m].astype(F32) + xr2[1, m].astype(F32)
        bbuf[m] = total.astype(BF16)
        return carry

    lax.fori_loop(0, ZH, x_sum, 0)
    for d in range(2):
        z_first(d).start()
    grads(0)
    rs_block(2)
    for d in range(2):
        z_first(d).wait_recv()
        to = z_side[d]["zh"]
        part = slice(32 * d, 32 * (d + 1))
        bbuf[to, :, part] = (bbuf[to, :, part].astype(F32) + zr1[d].astype(F32)).astype(BF16)
        z_second(d).start()

    for kk in range(ZL):
        acc0[...] = share(far(kk) * Y + y)
        for d in range(2):
            rs_full(d, 2, kk).wait_recv()
        total = acc0[...] + rs_in[0, 2, kk].astype(F32) + rs_in[1, 2, kk].astype(F32)
        if kk < 2:
            tz_out[kk] = total.astype(BF16)
            rs_z(kk).start()
        else:
            acc0[...] = total
    grads(1)
    for j in range(2):
        rs_z(j).wait_recv()
    gi_ref[...] = (acc0[...] + tz_in[0].astype(F32) + tz_in[1].astype(F32)).astype(BF16)
    for d in range(2):
        z_second(d).wait_recv()
    total = bbuf[zh].astype(F32) + zr2[0].astype(F32) + zr2[1].astype(F32)
    gw_ref[...] = (total * F32(1.0 / (ZH * X * C))).reshape(192, B)

    for j in range(2):
        ag_z(j, me).wait_send()
        rs_z(j).wait_send()
    for d in range(2):
        x_first(d).wait_send()
        x_second(d).wait_send()
        z_first(d).wait_send()
        z_second(d).wait_send()

    def sent(kk, carry):
        for d in range(2):
            for s in range(3):
                ag_full(d, s, kk, me).wait_send()
                rs_full(d, s, kk).wait_send()
            ag_half(d, kk, me).wait_send()
            rs_half(d, kk).wait_send()
        return carry

    lax.fori_loop(0, ZL, sent, 0)

    def pair_sent(i, carry):
        c_send(i).wait_send()
        return carry

    lax.fori_loop(0, ZH * X, pair_sent, 0)


def on_device(saved_input, queries, keys, value_weight, grad_attended):
    hbm = pl.BlockSpec(memory_space=pltpu.HBM)
    vmem = pl.BlockSpec(memory_space=pltpu.VMEM)
    dma = pltpu.SemaphoreType.DMA
    outs = pl.pallas_call(
        kernel,
        out_shape=(
            jax.ShapeDtypeStruct((B, B), BF16),
            jax.ShapeDtypeStruct((192, B), F32),
            jax.ShapeDtypeStruct((B, B), BF16),
            jax.ShapeDtypeStruct((B, B), BF16),
        ),
        in_specs=[hbm] * 5,
        out_specs=(vmem,) * 4,
        scratch_shapes=[
            pltpu.VMEM((T, B, B), BF16),
            pltpu.VMEM((T * B, B), BF16),
            pltpu.VMEM((B, B), BF16),
            pltpu.VMEM((B, B), BF16),
            pltpu.VMEM((B, B), BF16),
            pltpu.VMEM((B, B), BF16),
            pltpu.VMEM((HEADS, B, B), F32),
            pltpu.VMEM((B, B), F32),
            pltpu.VMEM((B, B), F32),
            pltpu.VMEM((B, B), F32),
            pltpu.VMEM((T * 4, 64, B), BF16),
            pltpu.VMEM((ZH * X, 3, 64, B), BF16),
            pltpu.VMEM((ZH, X, 3, 64, B), BF16),
            pltpu.VMEM((2, 2, 3, 64, B), BF16),
            pltpu.VMEM((2, ZH, 3, 64, B), BF16),
            pltpu.VMEM((ZH, 3, 64, B), BF16),
            pltpu.VMEM((2, 3, 32, B), BF16),
            pltpu.VMEM((2, 3, 64, B), BF16),
            pltpu.VMEM((2, ZL, H, B), BF16),
            pltpu.VMEM((2, ZL, H, B), BF16),
            pltpu.VMEM((2, 3, ZL, B, B), BF16),
            pltpu.VMEM((2, 3, ZL, B, B), BF16),
            pltpu.VMEM((2, B, B), BF16),
            pltpu.VMEM((2, B, B), BF16),
            dma((5,)),
            dma((2,)), dma((2,)),
            dma((2, 4, ZL)), dma((2, 4, ZL)),
            dma((2, 4, ZL)), dma((2, 4, ZL)),
            dma((2,)), dma((2,)),
            dma((ZH * X,)), dma((ZH * X,)),
            dma((2,)), dma((2,)), dma((2,)), dma((2,)),
            dma((2,)), dma((2,)), dma((2,)), dma((2,)),
        ],
        compiler_params=pltpu.CompilerParams(
            collective_id=0, has_side_effects=True, vmem_limit_bytes=48 * 1024 * 1024
        ),
    )(saved_input, queries, keys, value_weight, grad_attended)
    return outs


def solution(mesh):
    torus = Mesh(mesh.devices.reshape(ZH, X, C, ZL, Y), AXES)
    rows, cols = ("zh", "x", "c"), ("zl", "y")
    placed = (P(rows, cols), P(rows, cols), P(rows, cols), P(None, cols), P(rows, cols))
    return jax.shard_map(
        on_device,
        mesh=torus,
        in_specs=placed,
        out_specs=(P(rows, cols),) * 4,
        check_vma=False,
    )
```

time: 292 us -> 99.6 us (0.34)
  waiting for transfers between devices: 225 us -> 0 us
  Pallas kernels: 0 us -> 90.6 us
  matrix products: 17.9 us -> 0 us
  local copies, waits for them, and re-layouts: 21.9 us -> 8.14 us
  between operations: 13.9 us -> 0.65 us
  blocking collectives: 12 us -> 0 us
    unnamed x5 -> x0, waiting for transfers between devices: 122 us -> none
    pallas_call x0 -> x1, Pallas kernels: none -> 90.6 us  [on_device(): pl.pallas_call(kernel, out_shape=(jax.ShapeDtypeStruct((B, B), BF16), jax...]
    reduce_scatter x2 -> x0, waiting for transfers between devices: 54.9 us -> none  [own_block(): pieces = lax.psum_scatter(pieces, axes[k], scatter_dimension=0, tiled=True)]
    all_gather x1 -> x0, waiting for transfers between devices: 48.5 us -> none  [all_blocks(): pieces = lax.all_gather(pieces, axes[k], axis=0, tiled=True)]
    dot_general x7 -> x0, matrix products: 16.7 us -> none  [the longest x1 4.53 us: on_device(): lax.dot_general(full_input, value_flat, (((0,), (0,)), ((), ())), preferr...]
    all_gather x1 -> x0, blocking collectives: 12 us -> none  [all_blocks(): pieces = lax.all_gather(pieces, axes[k], axis=0, tiled=True)]
    transpose x2 -> x0, local copies, waits for them, and re-layouts: 8.55 us -> none  [the longest x1 4.73 us: in_order(): pieces = jnp.moveaxis(pieces, 0, dim)]
    reshape x3 -> x0, local copies, waits for them, and re-layouts: 4.38 us -> none  [the longest x1 2.37 us: own_block(): pieces = pieces.reshape(*(lax.axis_size(a) for a in axes), *inside)]
  transfers between devices with their start and end apart: 4 -> 0, of which waited for: 4 -> 0; matrix products, arithmetic and copies ran while one was open for 14% -> 0% of each run, Pallas kernels for 0% -> 0%
where the time goes in v1:
time: 99.6 us; the launch traced here: 99.4 us
  Pallas kernels  90.6 us (91%)
  local copies, waits for them, and re-layouts  8.14 us (8%)
    pallas_call x1, Pallas kernels, on_device(): pl.pallas_call(kernel, out_shape=(jax.ShapeDtypeStruct((B, B), BF16), jax...  90.6 us
    unnamed x14, local copies, waits for them, and re-layouts  8.14 us

profile of v1, /device:TPU:1, one launch (start us, length us, event | category | flops | bytes accessed | tf_op | source)
XLA Modules:
  0.0 99.4 jit_solution(15862096928628253448)
XLA Ops:
  0.6 0.0 copy-start
  0.6 1.9 %copy-done = bf16[6144,256]{1,0:T(8,128)(2,1)S(1)} copy-done((bf16[6144,256]{1,0:T(8,128)(2,1)S(1)}, bf16[6144,256]{1,0:T(8,128)(2,1)}, u32[]{:S(2)}) %copy-start) | copy-done | bytes 3145752
  2.5 0.0 copy-start.1
  2.5 0.9 copy-done.1
  3.4 0.0 copy-start.2
  3.4 0.9 copy-done.2
  4.3 0.0 copy-start.3
  4.3 0.9 copy-done.3
  5.2 0.0 copy-start.4
  5.2 0.9 copy-done.4
  6.1 90.6 %shard_map.84 = (bf16[256,256]{1,0:T(8,128)(2,1)S(1)}, f32[192,256]{1,0:T(8,128)S(1)}, bf16[256,256]{1,0:T(8,128)(2,1)S(1)}, bf16[256,256]{1,0:T(8,128)(2,1)S(1)}) custom-call(bf16[256,256]{1,0:T(8,128)(2,1)S(1)} %copy-done.1, bf16[256,256]{1,0:T(8,128)(2,1)S(1)} %copy-done.2, bf16[256,256]{1,0:T(8,128)(2,1)S(1)} %copy-done.3, ...), custom_call_target="tpu_custom_call" | custom-call | tf_op jit(solution)/shard_map/pallas_call | solution.py:343
  96.8 0.7 copy.13
  97.4 0.7 copy.14
  98.1 0.7 copy.15
  98.8 0.7 copy.16
Async XLA Ops:
  0.6 1.9 %copy-start = (bf16[6144,256]{1,0:T(8,128)(2,1)S(1)}, bf16[6144,256]{1,0:T(8,128)(2,1)}, u32[]{:S(2)}) copy-start(bf16[6144,256]{1,0:T(8,128)(2,1)} %w_hbm.1) | copy-start | bytes 9437188
  2.5 0.9 copy-start.1
  3.4 0.9 copy-start.2
  4.3 0.9 copy-start.3
  5.2 0.9 copy-start.4

commit v2 on v1

v2 whole, which is shorter than its diff:
```python
import math

import jax
import jax.numpy as jnp
from jax import lax
from jax.experimental import pallas as pl
from jax.experimental.pallas import tpu as pltpu
from jax.sharding import Mesh
from jax.sharding import PartitionSpec as P

HD = 128
HEADS = 2
ZH, X, C, ZL, Y = 4, 4, 2, 3, 8
AXES = ("zh", "x", "c", "zl", "y")
T = ZL * Y
B = 256
H = B // 2
RA = 160
MESH = pl.DeviceIdType.MESH
F32 = jnp.float32
BF16 = jnp.bfloat16
SCALE = 1.0 / math.sqrt(HD)


def dot(a, b, ca, cb):
    return lax.dot_general(a, b, (((ca,), (cb,)), ((), ())), preferred_element_type=F32)


def kernel(
    x_hbm, q_hbm, k_hbm, w_hbm, ga_hbm,
    gi_ref, gw_ref, gq_ref, gk_ref,
    xall, w, q, k, ga, gv, att, vals, acc0, acc1,
    wt, crecv, abuf, xr1, xr2, bbuf, zr1, zr2,
    s4_out, s4_in, rs_out, rs_in, tz_out, tz_in,
    in_sem, agz_s, agz_r, agb_s, agb_r, ag_s, ag_r, rs_s, rs_r, tz_s, tz_r,
    c_s, c_r, x1_s, x1_r, x2_s, x2_r, z1_s, z1_r, z2_s, z2_r,
):
    zh, xx, c, zl, y = (lax.axis_index(a) for a in AXES)
    me = zl * Y + y
    acc = (acc0, acc1)

    def up(value, step, size):
        return lax.rem(value + (step + size), size)

    ahead = ({"y": up(y, 1, Y)}, {"y": up(y, -1, Y)})
    x_side = ({"x": up(xx, 1, X)}, {"x": up(xx, -1, X)})
    z_side = ({"zh": up(zh, 1, ZH)}, {"zh": up(zh, -1, ZH)})
    plane = ({"zl": up(zl, 1, ZL)}, {"zl": up(zl, 2, ZL)})
    partner = {"c": 1 - c}

    def remote(src, dst, send, recv, where):
        return pltpu.make_async_remote_copy(
            src_ref=src, dst_ref=dst, send_sem=send, recv_sem=recv,
            device_id=where, device_id_type=MESH,
        )

    loads = [
        pltpu.make_async_copy(x_hbm, xall.at[me], in_sem.at[0]),
        pltpu.make_async_copy(q_hbm, q, in_sem.at[1]),
        pltpu.make_async_copy(k_hbm, k, in_sem.at[2]),
        pltpu.make_async_copy(ga_hbm, ga, in_sem.at[3]),
        pltpu.make_async_copy(w_hbm, w, in_sem.at[4]),
    ]
    for load in loads:
        load.start()

    barrier = pltpu.get_barrier_semaphore()
    friends = (*ahead, *x_side, *z_side, *plane, partner)
    for friend in friends:
        pl.semaphore_signal(barrier, inc=1, device_id=friend, device_id_type=MESH)
    pl.semaphore_wait(barrier, len(friends))

    def near(kk):
        return up(zl, -kk, ZL)

    def ag_y(d, s, kk, t):
        n = B if kk == 0 else RA
        part = pl.ds(d * (n // 2), n // 2) if s == 3 else pl.ds(0, n)
        ref = xall.at[t, part]
        return remote(ref, ref, ag_s.at[d, s, kk], ag_r.at[d, s, kk], ahead[d])

    def ag_z(j, t):
        ref = xall.at[t, pl.ds(0, RA)]
        return remote(ref, ref, agz_s.at[j], agz_r.at[j], plane[j])

    def ag_b(j, m, t):
        ref = xall.at[t, pl.ds(RA, B - RA)]
        return remote(ref, ref, agb_s.at[j, m], agb_r.at[j, m], plane[j])

    loads[0].wait()
    for j in range(2):
        ag_z(j, me).start()
    for d in range(2):
        ag_y(d, 0, 0, me).start()
    for j in range(2):
        ag_b(j, 0, me).start()

    row = lax.broadcasted_iota(jnp.int32, (B, B), 0)
    col = lax.broadcasted_iota(jnp.int32, (B, B), 1)
    for load in loads[1:4]:
        load.wait()

    def probs(h):
        cols = slice(h * HD, (h + 1) * HD)
        scores = dot(q[:, cols], k[:, cols], 1, 1) * SCALE
        scores = jnp.where(row >= col, scores, -jnp.inf)
        e = jnp.exp(scores - jnp.max(scores, axis=-1, keepdims=True))
        a = e / jnp.sum(e, axis=-1, keepdims=True)
        att[h] = a
        gv[:, cols] = dot(a.astype(BF16), ga[:, cols], 0, 0).astype(BF16)

    probs(0)
    for j in range(2):
        t = near(j + 1) * Y + y
        ag_z(j, t).wait_recv()
        for d in range(2):
            ag_y(d, 0, j + 1, t).start()
    probs(1)
    vals[...] = jnp.zeros_like(vals)
    loads[4].wait()

    def consume(t):
        rows = pl.ds(pl.multiple_of(t * B, B), B)
        vals[...] += dot(xall[t], w[rows], 1, 0)
        term = dot(xall[t], gv[...], 0, 0).astype(BF16)
        wt[pl.ds(t * 4, 4)] = term.reshape(4, 64, B)

    def consume_at(kk, m):
        t = near(kk) * Y + up(y, m, Y)
        if kk:
            ag_b(kk - 1, m, t).wait_recv()
        consume(t)

    def far(kk):
        return up(zl, kk + 1, ZL)

    def share(t):
        rows = pl.ds(pl.multiple_of(t * B, B), B)
        return dot(gv[...], w[rows], 1, 1)

    def rs_half(d, kk):
        return remote(
            s4_out.at[d, kk], s4_in.at[d, kk], rs_s.at[d, 0, kk], rs_r.at[d, 0, kk], ahead[d]
        )

    def rs_full(d, n, kk):
        return remote(
            rs_out.at[d, n, kk], rs_in.at[d, n, kk],
            rs_s.at[d, n + 1, kk], rs_r.at[d, n + 1, kk], ahead[d],
        )

    def rs_z(j):
        return remote(tz_out.at[j], tz_in.at[j], tz_s.at[j], tz_r.at[j], plane[j])

    def rs_first(kk, carry):
        p = share(far(kk) * Y + up(y, 4, Y)).astype(BF16)
        for d in range(2):
            s4_out[d, kk] = p[d * H : (d + 1) * H]
            rs_half(d, kk).start()
        return carry

    def ring(s, carry):
        reach = (Y - 1 - s, s + 1)
        before = (lax.rem(Y - s, Y), s)
        for kk in range(ZL):
            for d in range(2):
                t = near(kk) * Y + up(y, reach[d], Y)
                for step in range(3):

                    @pl.when(s == step)
                    def _():
                        ag_y(d, step, kk, t).wait_recv()
                        ag_y(d, step + 1, kk, t).start()

                if kk == 0:
                    for j in range(2):
                        ag_b(j, reach[d], t).start()
            if kk < 2:
                consume_at(kk + 1, before[0])

                @pl.when(s > 0)
                def _():
                    consume_at(kk + 1, before[1])
            else:
                for d in range(2):
                    consume_at(0, reach[d])

                @pl.when(s == 0)
                def _():
                    consume_at(0, 0)
        return carry

    lax.fori_loop(0, 3, ring, 0)

    def rs_chunk(n, kk):
        step = 3 - n
        for d in range(2):
            acc[d][...] = share(far(kk) * Y + up(y, step if d == 0 else -step, Y))
        for d in range(2):
            if n == 0:
                rs_half(d, kk).wait_recv()
                part = slice(d * H, (d + 1) * H)
                acc[d][part] += s4_in[d, kk].astype(F32)
                rs_out[d, n, kk] = acc[d][...].astype(BF16)
            else:
                rs_full(d, n - 1, kk).wait_recv()
                rs_out[d, n, kk] = (acc[d][...] + rs_in[d, n - 1, kk].astype(F32)).astype(BF16)
            rs_full(d, n, kk).start()

    def arrived(kk):
        t = near(kk) * Y + up(y, 4, Y)
        for d in range(2):
            ag_y(d, 3, kk, t).wait_recv()
        if kk == 0:
            for j in range(2):
                ag_b(j, 4, t).start()

    lax.fori_loop(0, ZL, rs_first, 0)
    arrived(0)
    for kk in (1, 2):
        for m in (5, 3):
            consume_at(kk, m)
    rs_chunk(0, 0)
    rs_chunk(0, 1)
    consume_at(0, 4)
    for kk in (1, 2):
        arrived(kk)
        consume_at(kk, 4)

    def c_send(i):
        other = (2 * i + 1 - c) * 3
        return remote(wt.at[pl.ds(other, 3)], crecv.at[i], c_s.at[i], c_r.at[i], partner)

    def x_first(h, d):
        return remote(
            abuf.at[h, pl.ds(2 * d, 2), up(xx, 2, X)], xr1.at[h, d],
            x1_s.at[h, d], x1_r.at[h, d], x_side[d],
        )

    def x_second(h, d):
        return remote(
            abuf.at[h, :, x_side[d]["x"]], xr2.at[h, d], x2_s.at[h, d], x2_r.at[h, d], x_side[d]
        )

    def z_first(h, d):
        return remote(
            bbuf.at[h, up(zh, 2, ZH), :, pl.ds(32 * d, 32)], zr1.at[h, d],
            z1_s.at[h, d], z1_r.at[h, d], z_side[d],
        )

    def z_second(h, d):
        return remote(
            bbuf.at[h, z_side[d]["zh"]], zr2.at[h, d], z2_s.at[h, d], z2_r.at[h, d], z_side[d]
        )

    def place(j):
        return lax.rem(j, ZH), up(xx, 2 + j // ZH, X)

    def cores(j, carry):
        m, to = place(j)
        c_send(m * X + to).start()
        return carry

    lax.fori_loop(0, ZH * X, cores, 0)

    def pair_sum(j, carry):
        m, to = place(j)
        i = m * X + to
        c_send(i).wait_recv()
        mine = wt[pl.ds((2 * i + c) * 3, 3)].astype(F32)
        pair = (mine + crecv[i].astype(F32)).astype(BF16)
        for h in range(2):
            abuf[h, m, to] = pair[:, :, h * H : (h + 1) * H]
        return carry

    lax.fori_loop(0, ZH, pair_sum, 0)
    for h in range(2):
        for d in range(2):
            x_first(h, d).start()
    rs_chunk(1, 0)
    rs_chunk(1, 1)
    lax.fori_loop(ZH, ZH * X, pair_sum, 0)

    def grads(h):
        cols = slice(h * HD, (h + 1) * HD)
        a = att[h]
        gp = dot(ga[:, cols], vals[:, cols].astype(BF16), 1, 1)
        rd = jnp.sum(a * gp, axis=-1, keepdims=True)
        gs = (a * (gp - rd) * SCALE).astype(BF16)
        gq_ref[:, cols] = dot(gs, k[:, cols], 1, 0).astype(BF16)
        gk_ref[:, cols] = dot(gs, q[:, cols], 0, 0).astype(BF16)

    def x_relay(h):
        for d in range(2):
            x_first(h, d).wait_recv()
            to = x_side[d]["x"]
            for half in range(2):
                m = 2 * d + half
                abuf[h, m, to] = (
                    abuf[h, m, to].astype(F32) + xr1[h, d, half].astype(F32)
                ).astype(BF16)
            x_second(h, d).start()

    def x_sum(h):
        for d in range(2):
            x_second(h, d).wait_recv()

        def body(m, carry):
            total = abuf[h, m, xx].astype(F32) + xr2[h, 0, m].astype(F32)
            bbuf[h, m] = (total + xr2[h, 1, m].astype(F32)).astype(BF16)
            return carry

        lax.fori_loop(0, ZH, body, 0)
        for d in range(2):
            z_first(h, d).start()

    def z_relay(h):
        for d in range(2):
            z_first(h, d).wait_recv()
            to = z_side[d]["zh"]
            part = slice(32 * d, 32 * (d + 1))
            bbuf[h, to, :, part] = (
                bbuf[h, to, :, part].astype(F32) + zr1[h, d].astype(F32)
            ).astype(BF16)
            z_second(h, d).start()

    def z_sum(h):
        for d in range(2):
            z_second(h, d).wait_recv()
        total = bbuf[h, zh].astype(F32) + zr2[h, 0].astype(F32) + zr2[h, 1].astype(F32)
        gw_ref[:, h * H : (h + 1) * H] = (total * F32(1.0 / (ZH * X * C))).reshape(192, H)

    def rs_last(kk):
        acc0[...] = share(far(kk) * Y + y)
        for d in range(2):
            rs_full(d, 2, kk).wait_recv()
        total = acc0[...] + rs_in[0, 2, kk].astype(F32) + rs_in[1, 2, kk].astype(F32)
        if kk < 2:
            tz_out[kk] = total.astype(BF16)
            rs_z(kk).start()
        else:
            acc0[...] = total

    rs_chunk(0, 2)
    x_relay(0)
    rs_chunk(2, 0)
    x_relay(1)
    rs_chunk(2, 1)
    grads(0)
    rs_chunk(1, 2)
    x_sum(0)
    rs_last(0)
    x_sum(1)
    rs_last(1)
    z_relay(0)
    rs_chunk(2, 2)
    grads(1)
    z_relay(1)
    rs_last(2)
    z_sum(0)
    for j in range(2):
        rs_z(j).wait_recv()
    gi_ref[...] = (acc0[...] + tz_in[0].astype(F32) + tz_in[1].astype(F32)).astype(BF16)

    z_sum(1)

    for j in range(2):
        ag_z(j, me).wait_send()
        rs_z(j).wait_send()
    for d in range(2):
        for h in range(2):
            x_first(h, d).wait_send()
            x_second(h, d).wait_send()
            z_first(h, d).wait_send()
            z_second(h, d).wait_send()

    for d in range(2):
        for kk in range(ZL):
            for s in range(4):
                ag_y(d, s, kk, me).wait_send()

    def b_sent(m, carry):
        for j in range(2):
            ag_b(j, m, me).wait_send()
        return carry

    lax.fori_loop(0, Y, b_sent, 0)

    def sent(kk, carry):
        for d in range(2):
            for s in range(3):
                rs_full(d, s, kk).wait_send()
            rs_half(d, kk).wait_send()
        return carry

    lax.fori_loop(0, ZL, sent, 0)

    def pair_sent(i, carry):
        c_send(i).wait_send()
        return carry

    lax.fori_loop(0, ZH * X, pair_sent, 0)


def on_device(saved_input, queries, keys, value_weight, grad_attended):
    hbm = pl.BlockSpec(memory_space=pltpu.HBM)
    vmem = pl.BlockSpec(memory_space=pltpu.VMEM)
    dma = pltpu.SemaphoreType.DMA
    outs = pl.pallas_call(
        kernel,
        out_shape=(
            jax.ShapeDtypeStruct((B, B), BF16),
            jax.ShapeDtypeStruct((192, B), F32),
            jax.ShapeDtypeStruct((B, B), BF16),
            jax.ShapeDtypeStruct((B, B), BF16),
        ),
        in_specs=[hbm] * 5,
        out_specs=(vmem,) * 4,
        scratch_shapes=[
            pltpu.VMEM((T, B, B), BF16),
            pltpu.VMEM((T * B, B), BF16),
            pltpu.VMEM((B, B), BF16),
            pltpu.VMEM((B, B), BF16),
            pltpu.VMEM((B, B), BF16),
            pltpu.VMEM((B, B), BF16),
            pltpu.VMEM((HEADS, B, B), F32),
            pltpu.VMEM((B, B), F32),
            pltpu.VMEM((B, B), F32),
            pltpu.VMEM((B, B), F32),
            pltpu.VMEM((T * 4, 64, B), BF16),
            pltpu.VMEM((ZH * X, 3, 64, B), BF16),
            pltpu.VMEM((2, ZH, X, 3, 64, H), BF16),
            pltpu.VMEM((2, 2, 2, 3, 64, H), BF16),
            pltpu.VMEM((2, 2, ZH, 3, 64, H), BF16),
            pltpu.VMEM((2, ZH, 3, 64, H), BF16),
            pltpu.VMEM((2, 2, 3, 32, H), BF16),
            pltpu.VMEM((2, 2, 3, 64, H), BF16),
            pltpu.VMEM((2, ZL, H, B), BF16),
            pltpu.VMEM((2, ZL, H, B), BF16),
            pltpu.VMEM((2, 3, ZL, B, B), BF16),
            pltpu.VMEM((2, 3, ZL, B, B), BF16),
            pltpu.VMEM((2, B, B), BF16),
            pltpu.VMEM((2, B, B), BF16),
            dma((5,)),
            dma((2,)), dma((2,)), dma((2, Y)), dma((2, Y)),
            dma((2, 4, ZL)), dma((2, 4, ZL)),
            dma((2, 4, ZL)), dma((2, 4, ZL)),
            dma((2,)), dma((2,)),
            dma((ZH * X,)), dma((ZH * X,)),
            dma((2, 2)), dma((2, 2)), dma((2, 2)), dma((2, 2)),
            dma((2, 2)), dma((2, 2)), dma((2, 2)), dma((2, 2)),
        ],
        compiler_params=pltpu.CompilerParams(
            collective_id=0, has_side_effects=True, vmem_limit_bytes=67_043_328
        ),
    )(saved_input, queries, keys, value_weight, grad_attended)
    return outs


def solution(mesh):
    torus = Mesh(mesh.devices.reshape(ZH, X, C, ZL, Y), AXES)
    rows, cols = ("zh", "x", "c"), ("zl", "y")
    placed = (P(rows, cols), P(rows, cols), P(rows, cols), P(None, cols), P(rows, cols))
    return jax.shard_map(
        on_device,
        mesh=torus,
        in_specs=placed,
        out_specs=(P(rows, cols),) * 4,
        check_vma=False,
    )
```

time: 99.6 us -> 91 us (0.914)
  Pallas kernels: 90.6 us -> 83.9 us
  local copies, waits for them, and re-layouts: 8.14 us -> 6.32 us
    pallas_call x1, Pallas kernels: 90.6 us -> 83.9 us  [on_device(): pl.pallas_call(kernel, out_shape=(jax.ShapeDtypeStruct((B, B), BF16), jax...]
    unnamed x14 -> x4, local copies, waits for them, and re-layouts: 8.14 us -> 6.32 us
where the time goes in v2:
time: 91 us; the launch traced here: 90.8 us
  Pallas kernels  83.9 us (92%)
  local copies, waits for them, and re-layouts  6.32 us (7%)
    pallas_call x1, Pallas kernels, on_device(): pl.pallas_call(kernel, out_shape=(jax.ShapeDtypeStruct((B, B), BF16), jax...  83.9 us
    unnamed x4, local copies, waits for them, and re-layouts  6.32 us

profile of v2, /device:TPU:1, one launch (start us, length us, event | category | flops | bytes accessed | tf_op | source)
XLA Modules:
  0.0 90.8 jit_solution(9927166176377563426)
XLA Ops:
  0.6 83.9 %shard_map.84 = (bf16[256,256]{1,0:T(8,128)(2,1)}, f32[192,256]{1,0:T(8,128)}, bf16[256,256]{1,0:T(8,128)(2,1)}, bf16[256,256]{1,0:T(8,128)(2,1)}) custom-call(bf16[256,256]{1,0:T(8,128)(2,1)} %x_hbm.1, bf16[256,256]{1,0:T(8,128)(2,1)} %q_hbm.1, bf16[256,256]{1,0:T(8,128)(2,1)} %k_hbm.1, bf16[6144,256]{1,0:T(8,128)(2,1)} %w_hbm.1, bf16[256,256]{1,0:T(8,128)(2,1)} %ga_hbm.1), custom_call_target="tpu_custom_call" | custom-call | tf_op jit(solution)/shard_map/pallas_call | solution.py:409
  84.5 1.6 %copy.13 = bf16[256,256]{1,0:T(8,128)(2,1)} copy(bf16[256,256]{1,0:T(8,128)(2,1)} %get-tuple-element.8) | data formatting | bytes 262144
  86.1 1.6 %copy.14 = f32[192,256]{1,0:T(8,128)} copy(f32[192,256]{1,0:T(8,128)} %get-tuple-element.9) | data formatting | bytes 393216
  87.7 1.6 %copy.15 = bf16[256,256]{1,0:T(8,128)(2,1)} copy(bf16[256,256]{1,0:T(8,128)(2,1)} %get-tuple-element.10) | data formatting | bytes 262144
  89.3 1.6 %copy.16 = bf16[256,256]{1,0:T(8,128)(2,1)} copy(bf16[256,256]{1,0:T(8,128)(2,1)} %get-tuple-element.11) | data formatting | bytes 262144

commit v3 on v2

--- a/solution.py
+++ b/solution.py
@@ -15,7 +15,7 @@
 T = ZL * Y
 B = 256
 H = B // 2
-RA = 160
+RA = 128
 MESH = pl.DeviceIdType.MESH
 F32 = jnp.float32
 BF16 = jnp.bfloat16
@@ -409,10 +409,10 @@
     outs = pl.pallas_call(
         kernel,
         out_shape=(
-            jax.ShapeDtypeStruct((B, B), BF16),
-            jax.ShapeDtypeStruct((192, B), F32),
-            jax.ShapeDtypeStruct((B, B), BF16),
-            jax.ShapeDtypeStruct((B, B), BF16),
+            pltpu.VMEM((B, B), BF16),
+            pltpu.VMEM((192, B), F32),
+            pltpu.VMEM((B, B), BF16),
+            pltpu.VMEM((B, B), BF16),
         ),
         in_specs=[hbm] * 5,
         out_specs=(vmem,) * 4,
@@ -451,7 +451,7 @@
             dma((2, 2)), dma((2, 2)), dma((2, 2)), dma((2, 2)),
         ],
         compiler_params=pltpu.CompilerParams(
-            collective_id=0, has_side_effects=True, vmem_limit_bytes=67_043_328
+            collective_id=0, has_side_effects=True, vmem_limit_bytes=66_400_000
         ),
     )(saved_input, queries, keys, value_weight, grad_attended)
     return outs

time: 91 us -> 84.8 us (0.932)
  local copies, waits for them, and re-layouts: 6.32 us -> 2.64 us
  Pallas kernels: 83.9 us -> 81 us
    unnamed x4, local copies, waits for them, and re-layouts: 6.32 us -> 2.64 us
    pallas_call x1, Pallas kernels: 83.9 us -> 81 us  [on_device(): pl.pallas_call(kernel, out_shape=(pltpu.VMEM((B, B), BF16), pltpu.VMEM((1...]
where the time goes in v3:
time: 84.8 us; the launch traced here: 84.3 us
  Pallas kernels  81 us (96%)
  local copies, waits for them, and re-layouts  2.64 us (3%)
    pallas_call x1, Pallas kernels, on_device(): pl.pallas_call(kernel, out_shape=(pltpu.VMEM((B, B), BF16), pltpu.VMEM((1...  81 us
    unnamed x4, local copies, waits for them, and re-layouts  2.64 us

profile of v3, /device:TPU:1, one launch (start us, length us, event | category | flops | bytes accessed | tf_op | source)
XLA Modules:
  0.0 84.3 jit_solution(2963746977059899753)
XLA Ops:
  0.6 81.0 %shard_map.84 = (bf16[256,256]{1,0:T(8,128)(2,1)S(1)}, f32[192,256]{1,0:T(8,128)S(1)}, bf16[256,256]{1,0:T(8,128)(2,1)S(1)}, bf16[256,256]{1,0:T(8,128)(2,1)S(1)}) custom-call(bf16[256,256]{1,0:T(8,128)(2,1)} %x_hbm.1, bf16[256,256]{1,0:T(8,128)(2,1)} %q_hbm.1, bf16[256,256]{1,0:T(8,128)(2,1)} %k_hbm.1, bf16[6144,256]{1,0:T(8,128)(2,1)} %w_hbm.1, ...), custom_call_target="tpu_custom_call" | custom-call | tf_op jit(solution)/shard_map/pallas_call | solution.py:409
  81.7 0.7 copy.13
  82.3 0.7 copy.15
  83.0 0.7 copy.16
  83.6 0.7 copy.14

commit v4 on v3

--- a/solution.py
+++ b/solution.py
@@ -400,6 +400,15 @@
         return carry
 
     lax.fori_loop(0, ZH * X, pair_sent, 0)
+
+
+def write_out(*refs):
+    sems = refs[8]
+    copies = [pltpu.make_async_copy(refs[n], refs[n + 4], sems.at[n]) for n in range(4)]
+    for copy in copies:
+        copy.start()
+    for copy in copies:
+        copy.wait()
 
 
 def on_device(saved_input, queries, keys, value_weight, grad_attended):
@@ -454,7 +463,14 @@
             collective_id=0, has_side_effects=True, vmem_limit_bytes=66_400_000
         ),
     )(saved_input, queries, keys, value_weight, grad_attended)
-    return outs
+    return pl.pallas_call(
+        write_out,
+        out_shape=tuple(jax.ShapeDtypeStruct(o.shape, o.dtype) for o in outs),
+        in_specs=[vmem] * 4,
+        out_specs=(hbm,) * 4,
+        scratch_shapes=[dma((4,))],
+        compiler_params=pltpu.CompilerParams(vmem_limit_bytes=1024 * 1024),
+    )(*outs)
 
 
 def solution(mesh):

time: 84.8 us -> 83 us (0.979)
  local copies, waits for them, and re-layouts: 2.64 us -> 0 us
  Pallas kernels: 81 us -> 81.9 us
    unnamed x4 -> x0, local copies, waits for them, and re-layouts: 2.64 us -> none
where the time goes in v4:
time: 83 us; the launch traced here: 82.5 us
  Pallas kernels  81.9 us (99%)
    pallas_call x1, Pallas kernels, on_device(): pl.pallas_call(kernel, out_shape=(pltpu.VMEM((B, B), BF16), pltpu.VMEM((1...  81 us

profile of v4, /device:TPU:1, one launch (start us, length us, event | category | flops | bytes accessed | tf_op | source)
XLA Modules:
  0.0 82.5 jit_solution(3814855011773752748)
XLA Ops:
  0.6 81.0 %shard_map.84 = (bf16[256,256]{1,0:T(8,128)(2,1)S(1)}, f32[192,256]{1,0:T(8,128)S(1)}, bf16[256,256]{1,0:T(8,128)(2,1)S(1)}, bf16[256,256]{1,0:T(8,128)(2,1)S(1)}) custom-call(bf16[256,256]{1,0:T(8,128)(2,1)} %x_hbm.1, bf16[256,256]{1,0:T(8,128)(2,1)} %q_hbm.1, bf16[256,256]{1,0:T(8,128)(2,1)} %k_hbm.1, bf16[6144,256]{1,0:T(8,128)(2,1)} %w_hbm.1, ...), custom_call_target="tpu_custom_call" | custom-call | tf_op jit(solution)/shard_map/pallas_call | solution.py:418
  81.7 0.8 %shard_map.85 = (bf16[256,256]{1,0:T(8,128)(2,1)}, f32[192,256]{1,0:T(8,128)}, bf16[256,256]{1,0:T(8,128)(2,1)}, bf16[256,256]{1,0:T(8,128)(2,1)}) custom-call(bf16[256,256]{1,0:T(8,128)(2,1)S(1)} %get-tuple-element.8.refs_0_, f32[192,256]{1,0:T(8,128)S(1)} %get-tuple-element.9.refs_1_, bf16[256,256]{1,0:T(8,128)(2,1)S(1)} %get-tuple-element.10.refs_2_, ...), custom_call_target="tpu_custom_call" | custom-call | tf_op jit(solution)/shard_map/pallas_call | solution.py:466
